TPU v7x, 256 devices: a whole 4x4x8 slice. The times are simulated.
256 devices in a mesh: tok: 32 (over z, y), head: 4 (over x), grp: 2 (over core).
Axes of the slice: x: 4, y: 4, z: 8, core: 2. Of those that a mesh axis runs over, the one named last changes fastest.
Arguments:
- tokens: bfloat16 [16384, 4096], P('tok', ('head', 'grp')), may hold values from -6 to 6
- norm_gain: bfloat16 [4096], P(('head', 'grp')), may hold values from 1.2 to 9, as said below
- query_key_value_weight: bfloat16 [4096, 6144], P(None, ('head', 'grp')), may hold values from -0.09375 to 0.09375
- out_weight: bfloat16 [4096, 4096], P(('head', 'grp')), may hold values from -0.09375 to 0.09375
- doc_ids: int32 [16384], P('tok'), may hold values from 0 to 15, never falling along the last dimension, each value on 1 to 8192 neighbouring positions
Outputs:
- attended: bfloat16 [16384, 4096], P('tok', ('head', 'grp'))
Inputs may be any that keep to these rules, and one draw needn't show every extreme that they name: `norm_gain`: norm gains are positive. `doc_ids`: non-decreasing along the window; each document has 1 to 8192 tokens and one has exactly 8192.
All inputs are finite; a program needn't handle non-finite values.
Results may differ from a plain program's by a relative error of at most 0.019.
The roundings to bfloat16 on the way count: a program that leaves them out, or rounds other values in their place, can miss the bound.
Values may be sent and summed in bfloat16 or wider, within the bound.
No kernel may reach another device: no remote copies, remote signals or barrier semaphores. Data moves between devices by JAX's collectives and lax.ppermute only.
A program may use at most 128 MiB of HBM per device.

v0:
```python
import jax
import jax.numpy as jnp
from jax import lax
from jax.sharding import PartitionSpec as P

QUERY_HEADS = 32
KEY_VALUE_HEADS = 8
HEAD_SIZE = 128
epsilon = 1e-05
theta = 500000.0
floor_score = -1e30


def rows_first(arrays, axis, dims):
    turned = [jnp.moveaxis(a, dim, 0) for a, dim in zip(arrays, dims)]
    both = jnp.concatenate([t.reshape(len(t), -1) for t in turned], axis=1)
    out, at, finished = (lax.all_gather(both, axis, axis=0, tiled=True), 0, [])
    for t, dim in zip(turned, dims):
        section = out[:, at : at + t[0].size].reshape(-1, *t.shape[1:])
        finished.append(jnp.moveaxis(section, 0, dim))
        at += t[0].size
    return tuple(finished)


def for_sending(array):

    def short(part):
        return part.astype(jnp.bfloat16) if part.dtype == jnp.float32 else part

    return jax.tree.map(short, array)


def passed_along(block, axis, distance):
    devices = range(lax.axis_size(axis))
    route = [((i - distance) % len(devices), i) for i in devices]
    return lax.ppermute(block, axis, route)


def rotate(vectors, positions):
    half = vectors.shape[-1] // 2
    inverse = 1.0 / theta ** (jnp.arange(half, dtype=jnp.float32) * (2.0 / vectors.shape[-1]))
    angles = positions.astype(jnp.float32)[:, None] * inverse[None, :]
    cosine = jnp.cos(angles)[:, None, :]
    sine = jnp.sin(angles)[:, None, :]
    first = vectors[..., :half]
    second = vectors[..., half:]
    return jnp.concatenate(
        [first * cosine - second * sine, second * cosine + first * sine], axis=-1
    )


def make_set(query_rows, positions, docs, head_group):
    length = query_rows.shape[0]
    flat = query_rows.reshape(length * head_group, query_rows.shape[1] // head_group)
    return (
        flat,
        jnp.repeat(positions, head_group),
        jnp.repeat(docs, head_group),
        docs[0],
        positions[length - 1],
    )


def empty_state(query_set):
    rows_all = query_set[0].shape[0]
    return (
        jnp.full((rows_all,), floor_score, jnp.float32),
        jnp.zeros((rows_all,), jnp.float32),
        jnp.zeros((rows_all, query_set[0].shape[1]), jnp.float32),
    )


def finish(state, head_group):
    highest, totals, accum = state
    normal = (accum / totals[:, None]).astype(jnp.bfloat16)
    return normal.reshape(normal.shape[0] // head_group, head_group * normal.shape[1])


def update(state, query_set, block_pairs, block_docs, block_positions):
    flat, query_positions, query_docs = (query_set[0], query_set[1], query_set[2])
    highest, totals, accum = state
    width = flat.shape[1]
    scores = lax.dot_general(
        flat, block_pairs[:, :width], (((1,), (1,)), ((), ())), preferred_element_type=jnp.float32
    ) * width ** (-0.5)
    mask = (block_positions[None, :] <= query_positions[:, None]) & (
        block_docs[None, :] == query_docs[:, None]
    )
    new_high = jnp.maximum(highest, jnp.max(jnp.where(mask, scores, floor_score), axis=1))
    weights = jnp.where(mask, jnp.exp(scores - new_high[:, None]), 0.0)
    fade = jnp.exp(highest - new_high)
    totals = totals * fade + jnp.sum(weights, axis=1)
    accum = accum * fade[:, None] + jnp.dot(
        weights.astype(jnp.bfloat16), block_pairs[:, width:], preferred_element_type=jnp.float32
    )
    return (new_high, totals, accum)


def fold_piece(state, query_set, pairs, docs, start):
    length = pairs.shape[0]
    width = 512

    def step(index, carried):
        offset = index * width
        first_key = start + offset
        block_positions = first_key + jnp.arange(width, dtype=jnp.int32)
        needed = (first_key <= query_set[4]) & (docs[width - 1] >= query_set[3])
        return lax.cond(
            needed,
            lambda held: update(held, query_set, pairs, docs, block_positions),
            lambda held: held,
            carried,
        )

    return lax.fori_loop(0, length // width, step, state)


def body(tokens, norm_gain, query_key_value_weight, out_weight, doc_ids):
    length = tokens.shape[0]
    head_group = QUERY_HEADS // KEY_VALUE_HEADS
    whole, gain = rows_first((tokens, norm_gain), ("head", "grp"), (1, 0))
    floats = whole.astype(jnp.float32)
    normed_input = (
        floats
        * lax.rsqrt(jnp.mean(floats * floats, axis=1, keepdims=True) + epsilon)
        * gain.astype(jnp.float32)
    ).astype(jnp.bfloat16)
    mixed_output = jnp.dot(normed_input, query_key_value_weight, preferred_element_type=jnp.float32)
    shard = lax.axis_index("tok")
    axis_size = lax.axis_size("tok")
    positions = shard * length + jnp.arange(length, dtype=jnp.int32)
    query_rows = (
        rotate(
            mixed_output[:, : head_group * HEAD_SIZE].reshape(length, head_group, HEAD_SIZE),
            positions,
        )
        .astype(jnp.bfloat16)
        .reshape(length, head_group * HEAD_SIZE)
    )
    keys = rotate(
        mixed_output[:, head_group * HEAD_SIZE : (head_group + 1) * HEAD_SIZE].reshape(
            length, 1, HEAD_SIZE
        ),
        positions,
    ).reshape(length, HEAD_SIZE)
    key_value = jnp.concatenate(
        [keys, mixed_output[:, (head_group + 1) * HEAD_SIZE :]], axis=1
    ).astype(jnp.bfloat16)
    query_sets = (make_set(query_rows, positions, doc_ids, head_group),)
    initial = tuple((empty_state(query_set) for query_set in query_sets))

    def fold_all(states, pieces, start):
        return tuple(
            (
                fold_piece(state, query_set, pieces[0], pieces[1], start)
                for state, query_set in zip(states, query_sets)
            )
        )

    reach = axis_size // 2
    first_states = fold_all(initial, (key_value, doc_ids), shard * length)

    def advance(step_index, carried):
        travelling, held = carried
        moved = jax.tree.map(
            lambda part, own: part.astype(own.dtype),
            passed_along(for_sending(travelling), "tok", 1),
            travelling,
        )
        anchor = jnp.mod(shard - step_index, axis_size)
        return (moved, fold_all(held, moved, anchor * length))

    states = lax.fori_loop(1, reach + 1, advance, ((key_value, doc_ids), first_states))[1]
    heads = finish(states[0], head_group)
    partial_products = jnp.dot(heads, out_weight, preferred_element_type=jnp.float32)
    return lax.psum_scatter(
        partial_products.astype(jnp.bfloat16), ("head", "grp"), scatter_dimension=1, tiled=True
    )


def solution(mesh):
    return jax.shard_map(
        body,
        mesh=mesh,
        in_specs=(
            P("tok", ("head", "grp")),
            P(("head", "grp")),
            P(None, ("head", "grp")),
            P(("head", "grp"), None),
            P("tok"),
        ),
        out_specs=P("tok", ("head", "grp")),
        check_vma=False,
    )
```

profile of v0, /device:TPU:8, one launch (start us, length us, event | category | flops | bytes accessed | tf_op | source)
XLA Modules:
  0.0 386.0 jit_solution(10557853256173840804)
XLA Ops:
  16.3 30.7 %all-gather.2.cloned.1.call-done = bf16[4096,513]{0,1:T(8,128)(2,1)} async-done(((bf16[512,513]{0,1:T(8,128)(2,1)}), bf16[4096,513]{0,1:T(8,128)(2,1)}) %all-gather.2.cloned.1.call-update) | async-done | bytes 4202512 | tf_op jit(solution)/shard_map/all_gather | solution.py:17
  51.0 7.2 %fusion.37 = f32[512,768]{1,0:T(8,128)S(1)} fusion(bf16[4096,768]{1,0:T(8,128)(2,1)} %param.13, f32[4096]{0:T(1024)S(1)} %bitcast.22, f32[512]{0:T(512)S(1)} %add_rsqrt_fusion, bf16[4096,513]{0,1:T(8,128)(2,1)} %all-gather.2.cloned.1.call-done), kind=kOutput, calls=%fused_computation.49 | convolution fusion | flops 3229614080 | bytes 12077056 | tf_op jit(solution)/shard_map/dot_general | solution.py:128
  64.9 5.6 %conditional.2 = ((f32[2048]{0:T(1024)S(1)}, f32[2048]{0:T(1024)S(1)}, f32[2048,128]{1,0:T(8,128)S(1)})) conditional(s32[]{:T(128)} %convert_element_type.61, (f32[2048]{0:T(1024)S(1)}, f32[2048]{0:T(1024)S(1)}, f32[2048,128]{1,0:T(8,128)S(1)}) %tuple.47, (s32[512]{0:T(512)S(1)}, s32[512]{0:T(512)S(1)}, s32[512]{0:T(512)S(1)}, s32[512]{0:T(512)S(1)}, ...), branch_computations={%region_1.2_spmd, %region_2.5_spmd} | conditional | flops 558370816 | bytes 16236576 | solution.py:108
  70.5 199.8 %while.46 = (s32[]{:T(128)}, bf16[512,256]{1,0:T(8,128)(2,1)S(1)}, s32[512]{0:T(512)S(1)}, f32[2048]{0:T(1024)S(1)}, f32[2048]{0:T(1024)S(1)}, /*index=5*/f32[20...) while((s32[]{:T(128)}, bf16[512,256]{1,0:T(8,128)(2,1)S(1)}, ...), condition=%wide.region_10.11_spmd.clone, body=%wide.region_5.10_spmd.clone.sunk | while | flops 558371328 | bytes 17304096 | solution.py:173
  74.0 5.1 %collective-permute-done.1 = s32[512]{0:T(512)S(1)} collective-permute-done((s32[512]{0:T(512)S(1)}, s32[512]{0:T(512)S(1)}, u32[]{:S(2)}, u32[]{:S(2)}) %collective-permute-start.1) | collective-permute-done | bytes 2080 | tf_op jit(solution)/shard_map/while/body/eval_jaxpr/ppermute | solution.py:36
  80.9 5.3 %conditional.5 = ((f32[2048]{0:T(1024)S(1)}, f32[2048]{0:T(1024)S(1)}, f32[2048,128]{1,0:T(8,128)S(1)})) conditional(s32[]{:T(128)} %convert_element_type.86, (f32[2048]{0:T(1024)S(1)}, f32[2048]{0:T(1024)S(1)}, f32[2048,128]{1,0:T(8,128)S(1)}) %tuple.76, (s32[]{:T(128)}, s32[512]{0:T(512)S(1)}, s32[512]{0:T(512)S(1)}, s32[512]{0:T(512)S(1)}, ...), branch_computations={%region_6.6_spmd, %region_7.9_spmd} | conditional | flops 558371328 | bytes 15716388 | solution.py:108
  89.6 4.3 %collective-permute-done.1 = s32[512]{0:T(512)S(1)} collective-permute-done((s32[512]{0:T(512)S(1)}, s32[512]{0:T(512)S(1)}, u32[]{:S(2)}, u32[]{:S(2)}) %collective-permute-start.1) | collective-permute-done | bytes 2080 | tf_op jit(solution)/shard_map/while/body/eval_jaxpr/ppermute | solution.py:36
  95.7 6.8 %collective-permute-start = (bf16[512,256]{1,0:T(8,128)(2,1)S(1)}, bf16[512,256]{1,0:T(8,128)(2,1)S(1)}, u32[]{:S(2)}, u32[]{:S(2)}) collective-permute-start(bf16[512,256]{1,0:T(8,128)(2,1)S(1)} %get-tuple-element.702), channel_id=1, source_target_pairs={{248,0},{0,8},{8,16},{16,24},{24,32},{32,40},{40,48},{48,56},{56,6... | collective-permute-start | bytes 786440 | tf_op jit(solution)/shard_map/while/body/eval_jaxpr/ppermute | solution.py:36
  112.2 4.7 %collective-permute-done.1 = s32[512]{0:T(512)S(1)} collective-permute-done((s32[512]{0:T(512)S(1)}, s32[512]{0:T(512)S(1)}, u32[]{:S(2)}, u32[]{:S(2)}) %collective-permute-start.1) | collective-permute-done | bytes 2080 | tf_op jit(solution)/shard_map/while/body/eval_jaxpr/ppermute | solution.py:36
  121.7 6.7 %collective-permute-done.1 = s32[512]{0:T(512)S(1)} collective-permute-done((s32[512]{0:T(512)S(1)}, s32[512]{0:T(512)S(1)}, u32[]{:S(2)}, u32[]{:S(2)}) %collective-permute-start.1) | collective-permute-done | bytes 2080 | tf_op jit(solution)/shard_map/while/body/eval_jaxpr/ppermute | solution.py:36
  133.6 6.4 %collective-permute-done.1 = s32[512]{0:T(512)S(1)} collective-permute-done((s32[512]{0:T(512)S(1)}, s32[512]{0:T(512)S(1)}, u32[]{:S(2)}, u32[]{:S(2)}) %collective-permute-start.1) | collective-permute-done | bytes 2080 | tf_op jit(solution)/shard_map/while/body/eval_jaxpr/ppermute | solution.py:36
  141.9 6.7 %collective-permute-start.1 = (s32[512]{0:T(512)S(1)}, s32[512]{0:T(512)S(1)}, u32[]{:S(2)}, u32[]{:S(2)}) collective-permute-start(s32[512]{0:T(512)S(1)} %get-tuple-element.703), channel_id=1, source_target_pairs={{248,0},{0,8},{8,16},{16,24},{24,32},{32,40},{40,48},{48,56},{56,6... | collective-permute-start | bytes 6152 | tf_op jit(solution)/shard_map/while/body/eval_jaxpr/ppermute | solution.py:36
  165.1 7.0 %collective-permute-start = (bf16[512,256]{1,0:T(8,128)(2,1)S(1)}, bf16[512,256]{1,0:T(8,128)(2,1)S(1)}, u32[]{:S(2)}, u32[]{:S(2)}) collective-permute-start(bf16[512,256]{1,0:T(8,128)(2,1)S(1)} %get-tuple-element.702), channel_id=1, source_target_pairs={{248,0},{0,8},{8,16},{16,24},{24,32},{32,40},{40,48},{48,56},{56,6... | collective-permute-start | bytes 786440 | tf_op jit(solution)/shard_map/while/body/eval_jaxpr/ppermute | solution.py:36
  184.2 4.9 %collective-permute-start.1 = (s32[512]{0:T(512)S(1)}, s32[512]{0:T(512)S(1)}, u32[]{:S(2)}, u32[]{:S(2)}) collective-permute-start(s32[512]{0:T(512)S(1)} %get-tuple-element.703), channel_id=1, source_target_pairs={{248,0},{0,8},{8,16},{16,24},{24,32},{32,40},{40,48},{48,56},{56,6... | collective-permute-start | bytes 6152 | tf_op jit(solution)/shard_map/while/body/eval_jaxpr/ppermute | solution.py:36
  192.5 4.7 %collective-permute-start = (bf16[512,256]{1,0:T(8,128)(2,1)S(1)}, bf16[512,256]{1,0:T(8,128)(2,1)S(1)}, u32[]{:S(2)}, u32[]{:S(2)}) collective-permute-start(bf16[512,256]{1,0:T(8,128)(2,1)S(1)} %get-tuple-element.702), channel_id=1, source_target_pairs={{248,0},{0,8},{8,16},{16,24},{24,32},{32,40},{40,48},{48,56},{56,6... | collective-permute-start | bytes 786440 | tf_op jit(solution)/shard_map/while/body/eval_jaxpr/ppermute | solution.py:36
  197.2 4.4 %collective-permute-start.1 = (s32[512]{0:T(512)S(1)}, s32[512]{0:T(512)S(1)}, u32[]{:S(2)}, u32[]{:S(2)}) collective-permute-start(s32[512]{0:T(512)S(1)} %get-tuple-element.703), channel_id=1, source_target_pairs={{248,0},{0,8},{8,16},{16,24},{24,32},{32,40},{40,48},{48,56},{56,6... | collective-permute-start | bytes 6152 | tf_op jit(solution)/shard_map/while/body/eval_jaxpr/ppermute | solution.py:36
  224.4 4.8 %collective-permute-done.1 = s32[512]{0:T(512)S(1)} collective-permute-done((s32[512]{0:T(512)S(1)}, s32[512]{0:T(512)S(1)}, u32[]{:S(2)}, u32[]{:S(2)}) %collective-permute-start.1) | collective-permute-done | bytes 2080 | tf_op jit(solution)/shard_map/while/body/eval_jaxpr/ppermute | solution.py:36
  236.2 4.4 %collective-permute-done.1 = s32[512]{0:T(512)S(1)} collective-permute-done((s32[512]{0:T(512)S(1)}, s32[512]{0:T(512)S(1)}, u32[]{:S(2)}, u32[]{:S(2)}) %collective-permute-start.1) | collective-permute-done | bytes 2080 | tf_op jit(solution)/shard_map/while/body/eval_jaxpr/ppermute | solution.py:36
  242.4 5.4 %collective-permute-start = (bf16[512,256]{1,0:T(8,128)(2,1)S(1)}, bf16[512,256]{1,0:T(8,128)(2,1)S(1)}, u32[]{:S(2)}, u32[]{:S(2)}) collective-permute-start(bf16[512,256]{1,0:T(8,128)(2,1)S(1)} %get-tuple-element.702), channel_id=1, source_target_pairs={{248,0},{0,8},{8,16},{16,24},{24,32},{32,40},{40,48},{48,56},{56,6... | collective-permute-start | bytes 786440 | tf_op jit(solution)/shard_map/while/body/eval_jaxpr/ppermute | solution.py:36
  247.7 5.1 %collective-permute-start.1 = (s32[512]{0:T(512)S(1)}, s32[512]{0:T(512)S(1)}, u32[]{:S(2)}, u32[]{:S(2)}) collective-permute-start(s32[512]{0:T(512)S(1)} %get-tuple-element.703), channel_id=1, source_target_pairs={{248,0},{0,8},{8,16},{16,24},{24,32},{32,40},{40,48},{48,56},{56,6... | collective-permute-start | bytes 6152 | tf_op jit(solution)/shard_map/while/body/eval_jaxpr/ppermute | solution.py:36
  256.0 5.5 %collective-permute-start = (bf16[512,256]{1,0:T(8,128)(2,1)S(1)}, bf16[512,256]{1,0:T(8,128)(2,1)S(1)}, u32[]{:S(2)}, u32[]{:S(2)}) collective-permute-start(bf16[512,256]{1,0:T(8,128)(2,1)S(1)} %get-tuple-element.702), channel_id=1, source_target_pairs={{248,0},{0,8},{8,16},{16,24},{24,32},{32,40},{40,48},{48,56},{56,6... | collective-permute-start | bytes 786440 | tf_op jit(solution)/shard_map/while/body/eval_jaxpr/ppermute | solution.py:36
  261.5 5.7 %collective-permute-start.1 = (s32[512]{0:T(512)S(1)}, s32[512]{0:T(512)S(1)}, u32[]{:S(2)}, u32[]{:S(2)}) collective-permute-start(s32[512]{0:T(512)S(1)} %get-tuple-element.703), channel_id=1, source_target_pairs={{248,0},{0,8},{8,16},{16,24},{24,32},{32,40},{40,48},{48,56},{56,6... | collective-permute-start | bytes 6152 | tf_op jit(solution)/shard_map/while/body/eval_jaxpr/ppermute | solution.py:36
  271.0 6.5 %convolution_convert_fusion = bf16[512,4096]{1,0:T(8,128)(2,1)} fusion(bf16[512,512]{1,0:T(8,128)(2,1)S(1)} %reshape.157, bf16[512,4096]{1,0:T(8,128)(2,1)} %param.14), kind=kOutput, calls=%fused_computation.48 | convolution fusion | flops 2149580800 | bytes 8912896 | tf_op jit(solution)/shard_map/dot_general | solution.py:175
  277.5 101.6 %reduce-scatter.2.cloned.1.call-done = bf16[512,512]{1,0:T(8,128)(2,1)} async-done(((bf16[512,4096]{1,0:T(8,128)(2,1)}), bf16[512,512]{1,0:T(8,128)(2,1)}) %reduce-scatter.2.cloned.1.call-update) | async-done | bytes 524304 | tf_op jit(solution)/shard_map/reduce_scatter | solution.py:176
  (194 shorter events, 101.3 us)
Async XLA Ops:
  6.5 40.5 %all-gather.2.cloned.1.call-start = ((), (), s32[]{:S(2)}) async-start(), calls=%async_computation.1 | async-start | bytes 4792320 | tf_op jit(solution)/shard_map/all_gather | solution.py:17
  9.1 370.0 %reduce-scatter.2.cloned.1.call-start = ((), (), s32[]{:S(2)}) async-start(), calls=%async_computation.2 | async-start | bytes 4718592 | tf_op jit(solution)/shard_map/reduce_scatter | solution.py:176
  70.5 10.3 %collective-permute-start = (bf16[512,256]{1,0:T(8,128)(2,1)S(1)}, bf16[512,256]{1,0:T(8,128)(2,1)S(1)}, u32[]{:S(2)}, u32[]{:S(2)}) collective-permute-start(bf16[512,256]{1,0:T(8,128)(2,1)S(1)} %get-tuple-element.702), channel_id=1, source_target_pairs={{248,0},{0,8},{8,16},{16,24},{24,32},{32,40},{40,48},{48,56},{56,6... | collective-permute-start | bytes 786440 | tf_op jit(solution)/shard_map/while/body/eval_jaxpr/ppermute | solution.py:36
  86.2 9.5 %collective-permute-start = (bf16[512,256]{1,0:T(8,128)(2,1)S(1)}, bf16[512,256]{1,0:T(8,128)(2,1)S(1)}, u32[]{:S(2)}, u32[]{:S(2)}) collective-permute-start(bf16[512,256]{1,0:T(8,128)(2,1)S(1)} %get-tuple-element.702), channel_id=1, source_target_pairs={{248,0},{0,8},{8,16},{16,24},{24,32},{32,40},{40,48},{48,56},{56,6... | collective-permute-start | bytes 786440 | tf_op jit(solution)/shard_map/while/body/eval_jaxpr/ppermute | solution.py:36
  95.7 12.9 %collective-permute-start = (bf16[512,256]{1,0:T(8,128)(2,1)S(1)}, bf16[512,256]{1,0:T(8,128)(2,1)S(1)}, u32[]{:S(2)}, u32[]{:S(2)}) collective-permute-start(bf16[512,256]{1,0:T(8,128)(2,1)S(1)} %get-tuple-element.702), channel_id=1, source_target_pairs={{248,0},{0,8},{8,16},{16,24},{24,32},{32,40},{40,48},{48,56},{56,6... | collective-permute-start | bytes 786440 | tf_op jit(solution)/shard_map/while/body/eval_jaxpr/ppermute | solution.py:36
  108.7 9.9 %collective-permute-start = (bf16[512,256]{1,0:T(8,128)(2,1)S(1)}, bf16[512,256]{1,0:T(8,128)(2,1)S(1)}, u32[]{:S(2)}, u32[]{:S(2)}) collective-permute-start(bf16[512,256]{1,0:T(8,128)(2,1)S(1)} %get-tuple-element.702), channel_id=1, source_target_pairs={{248,0},{0,8},{8,16},{16,24},{24,32},{32,40},{40,48},{48,56},{56,6... | collective-permute-start | bytes 786440 | tf_op jit(solution)/shard_map/while/body/eval_jaxpr/ppermute | solution.py:36
  118.7 11.4 %collective-permute-start = (bf16[512,256]{1,0:T(8,128)(2,1)S(1)}, bf16[512,256]{1,0:T(8,128)(2,1)S(1)}, u32[]{:S(2)}, u32[]{:S(2)}) collective-permute-start(bf16[512,256]{1,0:T(8,128)(2,1)S(1)} %get-tuple-element.702), channel_id=1, source_target_pairs={{248,0},{0,8},{8,16},{16,24},{24,32},{32,40},{40,48},{48,56},{56,6... | collective-permute-start | bytes 786440 | tf_op jit(solution)/shard_map/while/body/eval_jaxpr/ppermute | solution.py:36
  119.5 8.9 %collective-permute-start.1 = (s32[512]{0:T(512)S(1)}, s32[512]{0:T(512)S(1)}, u32[]{:S(2)}, u32[]{:S(2)}) collective-permute-start(s32[512]{0:T(512)S(1)} %get-tuple-element.703), channel_id=1, source_target_pairs={{248,0},{0,8},{8,16},{16,24},{24,32},{32,40},{40,48},{48,56},{56,6... | collective-permute-start | bytes 6152 | tf_op jit(solution)/shard_map/while/body/eval_jaxpr/ppermute | solution.py:36
  130.2 11.5 %collective-permute-start = (bf16[512,256]{1,0:T(8,128)(2,1)S(1)}, bf16[512,256]{1,0:T(8,128)(2,1)S(1)}, u32[]{:S(2)}, u32[]{:S(2)}) collective-permute-start(bf16[512,256]{1,0:T(8,128)(2,1)S(1)} %get-tuple-element.702), channel_id=1, source_target_pairs={{248,0},{0,8},{8,16},{16,24},{24,32},{32,40},{40,48},{48,56},{56,6... | collective-permute-start | bytes 786440 | tf_op jit(solution)/shard_map/while/body/eval_jaxpr/ppermute | solution.py:36
  130.3 9.7 %collective-permute-start.1 = (s32[512]{0:T(512)S(1)}, s32[512]{0:T(512)S(1)}, u32[]{:S(2)}, u32[]{:S(2)}) collective-permute-start(s32[512]{0:T(512)S(1)} %get-tuple-element.703), channel_id=1, source_target_pairs={{248,0},{0,8},{8,16},{16,24},{24,32},{32,40},{40,48},{48,56},{56,6... | collective-permute-start | bytes 6152 | tf_op jit(solution)/shard_map/while/body/eval_jaxpr/ppermute | solution.py:36
  141.8 11.5 %collective-permute-start = (bf16[512,256]{1,0:T(8,128)(2,1)S(1)}, bf16[512,256]{1,0:T(8,128)(2,1)S(1)}, u32[]{:S(2)}, u32[]{:S(2)}) collective-permute-start(bf16[512,256]{1,0:T(8,128)(2,1)S(1)} %get-tuple-element.702), channel_id=1, source_target_pairs={{248,0},{0,8},{8,16},{16,24},{24,32},{32,40},{40,48},{48,56},{56,6... | collective-permute-start | bytes 786440 | tf_op jit(solution)/shard_map/while/body/eval_jaxpr/ppermute | solution.py:36
  141.9 9.7 %collective-permute-start.1 = (s32[512]{0:T(512)S(1)}, s32[512]{0:T(512)S(1)}, u32[]{:S(2)}, u32[]{:S(2)}) collective-permute-start(s32[512]{0:T(512)S(1)} %get-tuple-element.703), channel_id=1, source_target_pairs={{248,0},{0,8},{8,16},{16,24},{24,32},{32,40},{40,48},{48,56},{56,6... | collective-permute-start | bytes 6152 | tf_op jit(solution)/shard_map/while/body/eval_jaxpr/ppermute | solution.py:36
  153.5 11.5 %collective-permute-start = (bf16[512,256]{1,0:T(8,128)(2,1)S(1)}, bf16[512,256]{1,0:T(8,128)(2,1)S(1)}, u32[]{:S(2)}, u32[]{:S(2)}) collective-permute-start(bf16[512,256]{1,0:T(8,128)(2,1)S(1)} %get-tuple-element.702), channel_id=1, source_target_pairs={{248,0},{0,8},{8,16},{16,24},{24,32},{32,40},{40,48},{48,56},{56,6... | collective-permute-start | bytes 786440 | tf_op jit(solution)/shard_map/while/body/eval_jaxpr/ppermute | solution.py:36
  165.1 15.2 %collective-permute-start = (bf16[512,256]{1,0:T(8,128)(2,1)S(1)}, bf16[512,256]{1,0:T(8,128)(2,1)S(1)}, u32[]{:S(2)}, u32[]{:S(2)}) collective-permute-start(bf16[512,256]{1,0:T(8,128)(2,1)S(1)} %get-tuple-element.702), channel_id=1, source_target_pairs={{248,0},{0,8},{8,16},{16,24},{24,32},{32,40},{40,48},{48,56},{56,6... | collective-permute-start | bytes 786440 | tf_op jit(solution)/shard_map/while/body/eval_jaxpr/ppermute | solution.py:36
  180.4 12.0 %collective-permute-start = (bf16[512,256]{1,0:T(8,128)(2,1)S(1)}, bf16[512,256]{1,0:T(8,128)(2,1)S(1)}, u32[]{:S(2)}, u32[]{:S(2)}) collective-permute-start(bf16[512,256]{1,0:T(8,128)(2,1)S(1)} %get-tuple-element.702), channel_id=1, source_target_pairs={{248,0},{0,8},{8,16},{16,24},{24,32},{32,40},{40,48},{48,56},{56,6... | collective-permute-start | bytes 786440 | tf_op jit(solution)/shard_map/while/body/eval_jaxpr/ppermute | solution.py:36
  192.5 13.3 %collective-permute-start = (bf16[512,256]{1,0:T(8,128)(2,1)S(1)}, bf16[512,256]{1,0:T(8,128)(2,1)S(1)}, u32[]{:S(2)}, u32[]{:S(2)}) collective-permute-start(bf16[512,256]{1,0:T(8,128)(2,1)S(1)} %get-tuple-element.702), channel_id=1, source_target_pairs={{248,0},{0,8},{8,16},{16,24},{24,32},{32,40},{40,48},{48,56},{56,6... | collective-permute-start | bytes 786440 | tf_op jit(solution)/shard_map/while/body/eval_jaxpr/ppermute | solution.py:36
  205.9 12.9 %collective-permute-start = (bf16[512,256]{1,0:T(8,128)(2,1)S(1)}, bf16[512,256]{1,0:T(8,128)(2,1)S(1)}, u32[]{:S(2)}, u32[]{:S(2)}) collective-permute-start(bf16[512,256]{1,0:T(8,128)(2,1)S(1)} %get-tuple-element.702), channel_id=1, source_target_pairs={{248,0},{0,8},{8,16},{16,24},{24,32},{32,40},{40,48},{48,56},{56,6... | collective-permute-start | bytes 786440 | tf_op jit(solution)/shard_map/while/body/eval_jaxpr/ppermute | solution.py:36
  209.3 7.7 %collective-permute-start.1 = (s32[512]{0:T(512)S(1)}, s32[512]{0:T(512)S(1)}, u32[]{:S(2)}, u32[]{:S(2)}) collective-permute-start(s32[512]{0:T(512)S(1)} %get-tuple-element.703), channel_id=1, source_target_pairs={{248,0},{0,8},{8,16},{16,24},{24,32},{32,40},{40,48},{48,56},{56,6... | collective-permute-start | bytes 6152 | tf_op jit(solution)/shard_map/while/body/eval_jaxpr/ppermute | solution.py:36
  218.9 12.1 %collective-permute-start = (bf16[512,256]{1,0:T(8,128)(2,1)S(1)}, bf16[512,256]{1,0:T(8,128)(2,1)S(1)}, u32[]{:S(2)}, u32[]{:S(2)}) collective-permute-start(bf16[512,256]{1,0:T(8,128)(2,1)S(1)} %get-tuple-element.702), channel_id=1, source_target_pairs={{248,0},{0,8},{8,16},{16,24},{24,32},{32,40},{40,48},{48,56},{56,6... | collective-permute-start | bytes 786440 | tf_op jit(solution)/shard_map/while/body/eval_jaxpr/ppermute | solution.py:36
  220.9 8.4 %collective-permute-start.1 = (s32[512]{0:T(512)S(1)}, s32[512]{0:T(512)S(1)}, u32[]{:S(2)}, u32[]{:S(2)}) collective-permute-start(s32[512]{0:T(512)S(1)} %get-tuple-element.703), channel_id=1, source_target_pairs={{248,0},{0,8},{8,16},{16,24},{24,32},{32,40},{40,48},{48,56},{56,6... | collective-permute-start | bytes 6152 | tf_op jit(solution)/shard_map/while/body/eval_jaxpr/ppermute | solution.py:36
  231.0 11.3 %collective-permute-start = (bf16[512,256]{1,0:T(8,128)(2,1)S(1)}, bf16[512,256]{1,0:T(8,128)(2,1)S(1)}, u32[]{:S(2)}, u32[]{:S(2)}) collective-permute-start(bf16[512,256]{1,0:T(8,128)(2,1)S(1)} %get-tuple-element.702), channel_id=1, source_target_pairs={{248,0},{0,8},{8,16},{16,24},{24,32},{32,40},{40,48},{48,56},{56,6... | collective-permute-start | bytes 786440 | tf_op jit(solution)/shard_map/while/body/eval_jaxpr/ppermute | solution.py:36
  231.5 9.0 %collective-permute-start.1 = (s32[512]{0:T(512)S(1)}, s32[512]{0:T(512)S(1)}, u32[]{:S(2)}, u32[]{:S(2)}) collective-permute-start(s32[512]{0:T(512)S(1)} %get-tuple-element.703), channel_id=1, source_target_pairs={{248,0},{0,8},{8,16},{16,24},{24,32},{32,40},{40,48},{48,56},{56,6... | collective-permute-start | bytes 6152 | tf_op jit(solution)/shard_map/while/body/eval_jaxpr/ppermute | solution.py:36
  242.4 13.5 %collective-permute-start = (bf16[512,256]{1,0:T(8,128)(2,1)S(1)}, bf16[512,256]{1,0:T(8,128)(2,1)S(1)}, u32[]{:S(2)}, u32[]{:S(2)}) collective-permute-start(bf16[512,256]{1,0:T(8,128)(2,1)S(1)} %get-tuple-element.702), channel_id=1, source_target_pairs={{248,0},{0,8},{8,16},{16,24},{24,32},{32,40},{40,48},{48,56},{56,6... | collective-permute-start | bytes 786440 | tf_op jit(solution)/shard_map/while/body/eval_jaxpr/ppermute | solution.py:36
  256.0 14.3 %collective-permute-start = (bf16[512,256]{1,0:T(8,128)(2,1)S(1)}, bf16[512,256]{1,0:T(8,128)(2,1)S(1)}, u32[]{:S(2)}, u32[]{:S(2)}) collective-permute-start(bf16[512,256]{1,0:T(8,128)(2,1)S(1)} %get-tuple-element.702), channel_id=1, source_target_pairs={{248,0},{0,8},{8,16},{16,24},{24,32},{32,40},{40,48},{48,56},{56,6... | collective-permute-start | bytes 786440 | tf_op jit(solution)/shard_map/while/body/eval_jaxpr/ppermute | solution.py:36
  (17 other events, 136.3 us)
Sparse Core Ops, SparseCore 0:
  9.2 37.7 all-gather.1
  277.6 101.4 reduce-scatter.1
where the time goes:
time: 387 us; the launch traced here: 386 us
  waiting for transfers between devices  187 us (48%)
  starting transfers between devices  99.6 us (26%)
  loops' own time  31 us (8%)
  matrix products  19.6 us (5%)
  local copies, waits for them, and re-layouts  18.7 us (5%)
  between operations  15.6 us (4%)
  other arithmetic  14.5 us (4%)
    reduce_scatter x1, waiting for transfers between devices, body(): lax.psum_scatter(partial_products.astype(jnp.bfloat16), ('head', 'grp'),...  102 us
    ppermute x32, starting transfers between devices, passed_along(): return lax.ppermute(block, axis, route)  99.5 us
    ppermute x32, waiting for transfers between devices, passed_along(): return lax.ppermute(block, axis, route)  54.7 us
    all_gather x1, waiting for transfers between devices, rows_first(): out, at, finished = (lax.all_gather(both, axis, axis=0, tiled=True), 0, [])  30.7 us
    another operation x1, loops' own time, body(): lax.fori_loop(1, reach + 1, advance, ((key_value, doc_ids), first_states))  30.4 us
    slice x16, local copies, waits for them, and re-layouts, step(): needed = (first_key <= query_set[4]) & (docs[width - 1] >= query_set[3])  9.34 us
  transfers between devices with their start and end apart: 34, of which 18 were waited for; matrix products, arithmetic and copies ran while one was open for 4% of the time, Pallas kernels for 0%

commit v1 on v0

--- a/solution.py
+++ b/solution.py
@@ -11,10 +11,15 @@
 floor_score = -1e30
 
 
+def exchange_gather(block, name, along):
+    stack = jnp.stack([block] * lax.axis_size(name))
+    return jnp.concatenate(lax.all_to_all(stack, name, 0, 0), axis=along)
+
+
 def rows_first(arrays, axis, dims):
     turned = [jnp.moveaxis(a, dim, 0) for a, dim in zip(arrays, dims)]
     both = jnp.concatenate([t.reshape(len(t), -1) for t in turned], axis=1)
-    out, at, finished = (lax.all_gather(both, axis, axis=0, tiled=True), 0, [])
+    out, at, finished = (exchange_gather(both, axis, 0), 0, [])
     for t, dim in zip(turned, dims):
         section = out[:, at : at + t[0].size].reshape(-1, *t.shape[1:])
         finished.append(jnp.moveaxis(section, 0, dim))

time: 387 us -> 407 us (1.052)
  waiting for transfers between devices: 187 us -> 225 us
  starting transfers between devices: 99.6 us -> 82.8 us
  local copies, waits for them, and re-layouts: 18.7 us -> 26.3 us
    all_to_all x0 -> x1, waiting for transfers between devices: none -> 44.3 us  [exchange_gather(): return jnp.concatenate(lax.all_to_all(stack, name, 0, 0), axis=along)]
    all_gather x1 -> x0, waiting for transfers between devices: 30.7 us -> none  [rows_first(): out, at, finished = (lax.all_gather(both, axis, axis=0, tiled=True), 0, [])]
    ppermute x32, waiting for transfers between devices: 54.7 us -> 78 us  [passed_along(): return lax.ppermute(block, axis, route)]
    ppermute x32, starting transfers between devices: 99.5 us -> 78.1 us  [passed_along(): return lax.ppermute(block, axis, route)]
    all_to_all x0 -> x1, starting transfers between devices: none -> 4.7 us  [exchange_gather(): return jnp.concatenate(lax.all_to_all(stack, name, 0, 0), axis=along)]
  transfers between devices with their start and end apart: 34 -> 34, of which waited for: 18 -> 18; matrix products, arithmetic and copies ran while one was open for 4% -> 3% of each run, Pallas kernels for 0% -> 0%
where the time goes in v1:
time: 407 us; the launch traced here: 406 us
  waiting for transfers between devices  225 us (55%)
  starting transfers between devices  82.8 us (20%)
  loops' own time  29.2 us (7%)
  local copies, waits for them, and re-layouts  26.3 us (6%)
  matrix products  16 us (4%)
  between operations  15.6 us (4%)
  other arithmetic  10.7 us (3%)
    reduce_scatter x1, waiting for transfers between devices, body(): lax.psum_scatter(partial_products.astype(jnp.bfloat16), ('head', 'grp'),...  103 us
    ppermute x32, starting transfers between devices, passed_along(): return lax.ppermute(block, axis, route)  78.1 us
    ppermute x32, waiting for transfers between devices, passed_along(): return lax.ppermute(block, axis, route)  78 us
    all_to_all x1, waiting for transfers between devices, exchange_gather(): return jnp.concatenate(lax.all_to_all(stack, name, 0, 0), axis=along)  44.3 us
    another operation x1, loops' own time, body(): lax.fori_loop(1, reach + 1, advance, ((key_value, doc_ids), first_states))  28.6 us
    slice x16, local copies, waits for them, and re-layouts, step(): needed = (first_key <= query_set[4]) & (docs[width - 1] >= query_set[3])  8.82 us
  transfers between devices with their start and end apart: 34, of which 18 were waited for; matrix products, arithmetic and copies ran while one was open for 3% of the time, Pallas kernels for 0%

profile of v1, /device:TPU:8, one launch (start us, length us, event | category | flops | bytes accessed | tf_op | source)
XLA Modules:
  0.0 405.8 jit_solution(15499870754857440148)
XLA Ops:
  10.6 4.7 %all-to-all-start = ((bf16[8,512,513]{1,2,0:T(8,128)(2,1)}), bf16[8,512,513]{1,2,0:T(8,128)(2,1)}, u32[]{:S(2)}, u32[]{:S(2)}) async-start(bf16[8,512,513]{1,2,0:T(8,128)(2,1)} %stack.2), calls=%async_computation | async-start | bytes 8519680 | tf_op jit(solution)/shard_map/all_to_all | solution.py:16
  21.4 44.3 %all-to-all-done = bf16[8,512,513]{1,2,0:T(8,128)(2,1)} async-done(((bf16[8,512,513]{1,2,0:T(8,128)(2,1)}), bf16[8,512,513]{1,2,0:T(8,128)(2,1)}, u32[]{:S(2)}, u32[]{:S(2)}) %all-to-all-start) | async-done | bytes 4202528 | tf_op jit(solution)/shard_map/all_to_all | solution.py:16
  83.7 5.6 %conditional.2 = ((f32[2048]{0:T(1024)S(1)}, f32[2048]{0:T(1024)S(1)}, f32[2048,128]{1,0:T(8,128)S(1)})) conditional(s32[]{:T(128)} %convert_element_type.61, (f32[2048]{0:T(1024)S(1)}, f32[2048]{0:T(1024)S(1)}, f32[2048,128]{1,0:T(8,128)S(1)}) %tuple.47, (s32[512]{0:T(512)S(1)}, s32[512]{0:T(512)S(1)}, s32[512]{0:T(512)S(1)}, s32[512]{0:T(512)S(1)}, ...), branch_computations={%region_1.2_spmd, %region_2.5_spmd} | conditional | flops 558370816 | bytes 16236576 | solution.py:113
  89.3 199.5 %while.46 = (s32[]{:T(128)}, bf16[512,256]{1,0:T(8,128)(2,1)S(1)}, s32[512]{0:T(512)S(1)}, f32[2048]{0:T(1024)S(1)}, f32[2048]{0:T(1024)S(1)}, /*index=5*/f32[20...) while((s32[]{:T(128)}, bf16[512,256]{1,0:T(8,128)(2,1)S(1)}, ...), condition=%wide.region_10.11_spmd.clone, body=%wide.region_5.10_spmd.clone.sunk | while | flops 558371328 | bytes 17304096 | solution.py:178
  92.8 4.8 %collective-permute-done.1 = s32[512]{0:T(512)S(1)} collective-permute-done((s32[512]{0:T(512)S(1)}, s32[512]{0:T(512)S(1)}, u32[]{:S(2)}, u32[]{:S(2)}) %collective-permute-start.1) | collective-permute-done | bytes 2080 | tf_op jit(solution)/shard_map/while/body/eval_jaxpr/ppermute | solution.py:41
  99.4 5.3 %conditional.5 = ((f32[2048]{0:T(1024)S(1)}, f32[2048]{0:T(1024)S(1)}, f32[2048,128]{1,0:T(8,128)S(1)})) conditional(s32[]{:T(128)} %convert_element_type.86, (f32[2048]{0:T(1024)S(1)}, f32[2048]{0:T(1024)S(1)}, f32[2048,128]{1,0:T(8,128)S(1)}) %tuple.76, (s32[]{:T(128)}, s32[512]{0:T(512)S(1)}, s32[512]{0:T(512)S(1)}, s32[512]{0:T(512)S(1)}, ...), branch_computations={%region_6.6_spmd, %region_7.9_spmd} | conditional | flops 558371328 | bytes 15716388 | solution.py:113
  113.9 6.2 %collective-permute-start = (bf16[512,256]{1,0:T(8,128)(2,1)S(1)}, bf16[512,256]{1,0:T(8,128)(2,1)S(1)}, u32[]{:S(2)}, u32[]{:S(2)}) collective-permute-start(bf16[512,256]{1,0:T(8,128)(2,1)S(1)} %get-tuple-element.702), channel_id=1, source_target_pairs={{248,0},{0,8},{8,16},{16,24},{24,32},{32,40},{40,48},{48,56},{56,6... | collective-permute-start | bytes 786440 | tf_op jit(solution)/shard_map/while/body/eval_jaxpr/ppermute | solution.py:41
  129.1 7.2 %collective-permute-done.1 = s32[512]{0:T(512)S(1)} collective-permute-done((s32[512]{0:T(512)S(1)}, s32[512]{0:T(512)S(1)}, u32[]{:S(2)}, u32[]{:S(2)}) %collective-permute-start.1) | collective-permute-done | bytes 2080 | tf_op jit(solution)/shard_map/while/body/eval_jaxpr/ppermute | solution.py:41
  139.3 8.6 %collective-permute-done.1 = s32[512]{0:T(512)S(1)} collective-permute-done((s32[512]{0:T(512)S(1)}, s32[512]{0:T(512)S(1)}, u32[]{:S(2)}, u32[]{:S(2)}) %collective-permute-start.1) | collective-permute-done | bytes 2080 | tf_op jit(solution)/shard_map/while/body/eval_jaxpr/ppermute | solution.py:41
  151.2 8.2 %collective-permute-done.1 = s32[512]{0:T(512)S(1)} collective-permute-done((s32[512]{0:T(512)S(1)}, s32[512]{0:T(512)S(1)}, u32[]{:S(2)}, u32[]{:S(2)}) %collective-permute-start.1) | collective-permute-done | bytes 2080 | tf_op jit(solution)/shard_map/while/body/eval_jaxpr/ppermute | solution.py:41
  161.4 4.9 %collective-permute-start.1 = (s32[512]{0:T(512)S(1)}, s32[512]{0:T(512)S(1)}, u32[]{:S(2)}, u32[]{:S(2)}) collective-permute-start(s32[512]{0:T(512)S(1)} %get-tuple-element.703), channel_id=1, source_target_pairs={{248,0},{0,8},{8,16},{16,24},{24,32},{32,40},{40,48},{48,56},{56,6... | collective-permute-start | bytes 6152 | tf_op jit(solution)/shard_map/while/body/eval_jaxpr/ppermute | solution.py:41
  177.3 6.1 %collective-permute-done.1 = s32[512]{0:T(512)S(1)} collective-permute-done((s32[512]{0:T(512)S(1)}, s32[512]{0:T(512)S(1)}, u32[]{:S(2)}, u32[]{:S(2)}) %collective-permute-start.1) | collective-permute-done | bytes 2080 | tf_op jit(solution)/shard_map/while/body/eval_jaxpr/ppermute | solution.py:41
  185.2 4.6 %collective-permute-start = (bf16[512,256]{1,0:T(8,128)(2,1)S(1)}, bf16[512,256]{1,0:T(8,128)(2,1)S(1)}, u32[]{:S(2)}, u32[]{:S(2)}) collective-permute-start(bf16[512,256]{1,0:T(8,128)(2,1)S(1)} %get-tuple-element.702), channel_id=1, source_target_pairs={{248,0},{0,8},{8,16},{16,24},{24,32},{32,40},{40,48},{48,56},{56,6... | collective-permute-start | bytes 786440 | tf_op jit(solution)/shard_map/while/body/eval_jaxpr/ppermute | solution.py:41
  189.8 5.0 %collective-permute-start.1 = (s32[512]{0:T(512)S(1)}, s32[512]{0:T(512)S(1)}, u32[]{:S(2)}, u32[]{:S(2)}) collective-permute-start(s32[512]{0:T(512)S(1)} %get-tuple-element.703), channel_id=1, source_target_pairs={{248,0},{0,8},{8,16},{16,24},{24,32},{32,40},{40,48},{48,56},{56,6... | collective-permute-start | bytes 6152 | tf_op jit(solution)/shard_map/while/body/eval_jaxpr/ppermute | solution.py:41
  203.1 4.3 %collective-permute-start.1 = (s32[512]{0:T(512)S(1)}, s32[512]{0:T(512)S(1)}, u32[]{:S(2)}, u32[]{:S(2)}) collective-permute-start(s32[512]{0:T(512)S(1)} %get-tuple-element.703), channel_id=1, source_target_pairs={{248,0},{0,8},{8,16},{16,24},{24,32},{32,40},{40,48},{48,56},{56,6... | collective-permute-start | bytes 6152 | tf_op jit(solution)/shard_map/while/body/eval_jaxpr/ppermute | solution.py:41
  219.6 5.3 %collective-permute-done.1 = s32[512]{0:T(512)S(1)} collective-permute-done((s32[512]{0:T(512)S(1)}, s32[512]{0:T(512)S(1)}, u32[]{:S(2)}, u32[]{:S(2)}) %collective-permute-start.1) | collective-permute-done | bytes 2080 | tf_op jit(solution)/shard_map/while/body/eval_jaxpr/ppermute | solution.py:41
  230.4 6.8 %collective-permute-done.1 = s32[512]{0:T(512)S(1)} collective-permute-done((s32[512]{0:T(512)S(1)}, s32[512]{0:T(512)S(1)}, u32[]{:S(2)}, u32[]{:S(2)}) %collective-permute-start.1) | collective-permute-done | bytes 2080 | tf_op jit(solution)/shard_map/while/body/eval_jaxpr/ppermute | solution.py:41
  242.6 6.1 %collective-permute-done.1 = s32[512]{0:T(512)S(1)} collective-permute-done((s32[512]{0:T(512)S(1)}, s32[512]{0:T(512)S(1)}, u32[]{:S(2)}, u32[]{:S(2)}) %collective-permute-start.1) | collective-permute-done | bytes 2080 | tf_op jit(solution)/shard_map/while/body/eval_jaxpr/ppermute | solution.py:41
  255.0 5.2 %collective-permute-done.1 = s32[512]{0:T(512)S(1)} collective-permute-done((s32[512]{0:T(512)S(1)}, s32[512]{0:T(512)S(1)}, u32[]{:S(2)}, u32[]{:S(2)}) %collective-permute-start.1) | collective-permute-done | bytes 2080 | tf_op jit(solution)/shard_map/while/body/eval_jaxpr/ppermute | solution.py:41
  266.2 4.8 %collective-permute-start.1 = (s32[512]{0:T(512)S(1)}, s32[512]{0:T(512)S(1)}, u32[]{:S(2)}, u32[]{:S(2)}) collective-permute-start(s32[512]{0:T(512)S(1)} %get-tuple-element.703), channel_id=1, source_target_pairs={{248,0},{0,8},{8,16},{16,24},{24,32},{32,40},{40,48},{48,56},{56,6... | collective-permute-start | bytes 6152 | tf_op jit(solution)/shard_map/while/body/eval_jaxpr/ppermute | solution.py:41
  274.2 5.0 %collective-permute-start = (bf16[512,256]{1,0:T(8,128)(2,1)S(1)}, bf16[512,256]{1,0:T(8,128)(2,1)S(1)}, u32[]{:S(2)}, u32[]{:S(2)}) collective-permute-start(bf16[512,256]{1,0:T(8,128)(2,1)S(1)} %get-tuple-element.702), channel_id=1, source_target_pairs={{248,0},{0,8},{8,16},{16,24},{24,32},{32,40},{40,48},{48,56},{56,6... | collective-permute-start | bytes 786440 | tf_op jit(solution)/shard_map/while/body/eval_jaxpr/ppermute | solution.py:41
  279.2 6.5 %collective-permute-start.1 = (s32[512]{0:T(512)S(1)}, s32[512]{0:T(512)S(1)}, u32[]{:S(2)}, u32[]{:S(2)}) collective-permute-start(s32[512]{0:T(512)S(1)} %get-tuple-element.703), channel_id=1, source_target_pairs={{248,0},{0,8},{8,16},{16,24},{24,32},{32,40},{40,48},{48,56},{56,6... | collective-permute-start | bytes 6152 | tf_op jit(solution)/shard_map/while/body/eval_jaxpr/ppermute | solution.py:41
  289.5 6.5 %convolution_convert_fusion = bf16[512,4096]{1,0:T(8,128)(2,1)} fusion(bf16[512,512]{1,0:T(8,128)(2,1)S(1)} %reshape.163, bf16[512,4096]{1,0:T(8,128)(2,1)} %param.14), kind=kOutput, calls=%fused_computation.48 | convolution fusion | flops 2149580800 | bytes 8912896 | tf_op jit(solution)/shard_map/dot_general | solution.py:180
  296.1 102.9 %reduce-scatter.2.cloned.1.call-done = bf16[512,512]{1,0:T(8,128)(2,1)} async-done(((bf16[512,4096]{1,0:T(8,128)(2,1)}), bf16[512,512]{1,0:T(8,128)(2,1)}) %reduce-scatter.2.cloned.1.call-update) | async-done | bytes 524304 | tf_op jit(solution)/shard_map/reduce_scatter | solution.py:181
  (204 shorter events, 103.3 us)
Async XLA Ops:
  10.6 55.0 %all-to-all-start = ((bf16[8,512,513]{1,2,0:T(8,128)(2,1)}), bf16[8,512,513]{1,2,0:T(8,128)(2,1)}, u32[]{:S(2)}, u32[]{:S(2)}) async-start(bf16[8,512,513]{1,2,0:T(8,128)(2,1)} %stack.2), calls=%async_computation | async-start | bytes 8519680 | tf_op jit(solution)/shard_map/all_to_all | solution.py:16
  15.3 383.6 %reduce-scatter.2.cloned.1.call-start = ((), (), s32[]{:S(2)}) async-start(), calls=%async_computation.2 | async-start | bytes 4718592 | tf_op jit(solution)/shard_map/reduce_scatter | solution.py:181
  89.4 10.0 %collective-permute-start = (bf16[512,256]{1,0:T(8,128)(2,1)S(1)}, bf16[512,256]{1,0:T(8,128)(2,1)S(1)}, u32[]{:S(2)}, u32[]{:S(2)}) collective-permute-start(bf16[512,256]{1,0:T(8,128)(2,1)S(1)} %get-tuple-element.702), channel_id=1, source_target_pairs={{248,0},{0,8},{8,16},{16,24},{24,32},{32,40},{40,48},{48,56},{56,6... | collective-permute-start | bytes 786440 | tf_op jit(solution)/shard_map/while/body/eval_jaxpr/ppermute | solution.py:41
  113.9 12.7 %collective-permute-start = (bf16[512,256]{1,0:T(8,128)(2,1)S(1)}, bf16[512,256]{1,0:T(8,128)(2,1)S(1)}, u32[]{:S(2)}, u32[]{:S(2)}) collective-permute-start(bf16[512,256]{1,0:T(8,128)(2,1)S(1)} %get-tuple-element.702), channel_id=1, source_target_pairs={{248,0},{0,8},{8,16},{16,24},{24,32},{32,40},{40,48},{48,56},{56,6... | collective-permute-start | bytes 786440 | tf_op jit(solution)/shard_map/while/body/eval_jaxpr/ppermute | solution.py:41
  126.7 11.3 %collective-permute-start = (bf16[512,256]{1,0:T(8,128)(2,1)S(1)}, bf16[512,256]{1,0:T(8,128)(2,1)S(1)}, u32[]{:S(2)}, u32[]{:S(2)}) collective-permute-start(bf16[512,256]{1,0:T(8,128)(2,1)S(1)} %get-tuple-element.702), channel_id=1, source_target_pairs={{248,0},{0,8},{8,16},{16,24},{24,32},{32,40},{40,48},{48,56},{56,6... | collective-permute-start | bytes 786440 | tf_op jit(solution)/shard_map/while/body/eval_jaxpr/ppermute | solution.py:41
  138.1 11.5 %collective-permute-start = (bf16[512,256]{1,0:T(8,128)(2,1)S(1)}, bf16[512,256]{1,0:T(8,128)(2,1)S(1)}, u32[]{:S(2)}, u32[]{:S(2)}) collective-permute-start(bf16[512,256]{1,0:T(8,128)(2,1)S(1)} %get-tuple-element.702), channel_id=1, source_target_pairs={{248,0},{0,8},{8,16},{16,24},{24,32},{32,40},{40,48},{48,56},{56,6... | collective-permute-start | bytes 786440 | tf_op jit(solution)/shard_map/while/body/eval_jaxpr/ppermute | solution.py:41
  138.2 9.7 %collective-permute-start.1 = (s32[512]{0:T(512)S(1)}, s32[512]{0:T(512)S(1)}, u32[]{:S(2)}, u32[]{:S(2)}) collective-permute-start(s32[512]{0:T(512)S(1)} %get-tuple-element.703), channel_id=1, source_target_pairs={{248,0},{0,8},{8,16},{16,24},{24,32},{32,40},{40,48},{48,56},{56,6... | collective-permute-start | bytes 6152 | tf_op jit(solution)/shard_map/while/body/eval_jaxpr/ppermute | solution.py:41
  149.7 11.5 %collective-permute-start = (bf16[512,256]{1,0:T(8,128)(2,1)S(1)}, bf16[512,256]{1,0:T(8,128)(2,1)S(1)}, u32[]{:S(2)}, u32[]{:S(2)}) collective-permute-start(bf16[512,256]{1,0:T(8,128)(2,1)S(1)} %get-tuple-element.702), channel_id=1, source_target_pairs={{248,0},{0,8},{8,16},{16,24},{24,32},{32,40},{40,48},{48,56},{56,6... | collective-permute-start | bytes 786440 | tf_op jit(solution)/shard_map/while/body/eval_jaxpr/ppermute | solution.py:41
  149.8 9.7 %collective-permute-start.1 = (s32[512]{0:T(512)S(1)}, s32[512]{0:T(512)S(1)}, u32[]{:S(2)}, u32[]{:S(2)}) collective-permute-start(s32[512]{0:T(512)S(1)} %get-tuple-element.703), channel_id=1, source_target_pairs={{248,0},{0,8},{8,16},{16,24},{24,32},{32,40},{40,48},{48,56},{56,6... | collective-permute-start | bytes 6152 | tf_op jit(solution)/shard_map/while/body/eval_jaxpr/ppermute | solution.py:41
  161.3 11.5 %collective-permute-start = (bf16[512,256]{1,0:T(8,128)(2,1)S(1)}, bf16[512,256]{1,0:T(8,128)(2,1)S(1)}, u32[]{:S(2)}, u32[]{:S(2)}) collective-permute-start(bf16[512,256]{1,0:T(8,128)(2,1)S(1)} %get-tuple-element.702), channel_id=1, source_target_pairs={{248,0},{0,8},{8,16},{16,24},{24,32},{32,40},{40,48},{48,56},{56,6... | collective-permute-start | bytes 786440 | tf_op jit(solution)/shard_map/while/body/eval_jaxpr/ppermute | solution.py:41
  161.4 9.7 %collective-permute-start.1 = (s32[512]{0:T(512)S(1)}, s32[512]{0:T(512)S(1)}, u32[]{:S(2)}, u32[]{:S(2)}) collective-permute-start(s32[512]{0:T(512)S(1)} %get-tuple-element.703), channel_id=1, source_target_pairs={{248,0},{0,8},{8,16},{16,24},{24,32},{32,40},{40,48},{48,56},{56,6... | collective-permute-start | bytes 6152 | tf_op jit(solution)/shard_map/while/body/eval_jaxpr/ppermute | solution.py:41
  172.9 12.2 %collective-permute-start = (bf16[512,256]{1,0:T(8,128)(2,1)S(1)}, bf16[512,256]{1,0:T(8,128)(2,1)S(1)}, u32[]{:S(2)}, u32[]{:S(2)}) collective-permute-start(bf16[512,256]{1,0:T(8,128)(2,1)S(1)} %get-tuple-element.702), channel_id=1, source_target_pairs={{248,0},{0,8},{8,16},{16,24},{24,32},{32,40},{40,48},{48,56},{56,6... | collective-permute-start | bytes 786440 | tf_op jit(solution)/shard_map/while/body/eval_jaxpr/ppermute | solution.py:41
  185.2 13.6 %collective-permute-start = (bf16[512,256]{1,0:T(8,128)(2,1)S(1)}, bf16[512,256]{1,0:T(8,128)(2,1)S(1)}, u32[]{:S(2)}, u32[]{:S(2)}) collective-permute-start(bf16[512,256]{1,0:T(8,128)(2,1)S(1)} %get-tuple-element.702), channel_id=1, source_target_pairs={{248,0},{0,8},{8,16},{16,24},{24,32},{32,40},{40,48},{48,56},{56,6... | collective-permute-start | bytes 786440 | tf_op jit(solution)/shard_map/while/body/eval_jaxpr/ppermute | solution.py:41
  199.0 14.5 %collective-permute-start = (bf16[512,256]{1,0:T(8,128)(2,1)S(1)}, bf16[512,256]{1,0:T(8,128)(2,1)S(1)}, u32[]{:S(2)}, u32[]{:S(2)}) collective-permute-start(bf16[512,256]{1,0:T(8,128)(2,1)S(1)} %get-tuple-element.702), channel_id=1, source_target_pairs={{248,0},{0,8},{8,16},{16,24},{24,32},{32,40},{40,48},{48,56},{56,6... | collective-permute-start | bytes 786440 | tf_op jit(solution)/shard_map/while/body/eval_jaxpr/ppermute | solution.py:41
  213.6 13.1 %collective-permute-start = (bf16[512,256]{1,0:T(8,128)(2,1)S(1)}, bf16[512,256]{1,0:T(8,128)(2,1)S(1)}, u32[]{:S(2)}, u32[]{:S(2)}) collective-permute-start(bf16[512,256]{1,0:T(8,128)(2,1)S(1)} %get-tuple-element.702), channel_id=1, source_target_pairs={{248,0},{0,8},{8,16},{16,24},{24,32},{32,40},{40,48},{48,56},{56,6... | collective-permute-start | bytes 786440 | tf_op jit(solution)/shard_map/while/body/eval_jaxpr/ppermute | solution.py:41
  215.2 9.7 %collective-permute-start.1 = (s32[512]{0:T(512)S(1)}, s32[512]{0:T(512)S(1)}, u32[]{:S(2)}, u32[]{:S(2)}) collective-permute-start(s32[512]{0:T(512)S(1)} %get-tuple-element.703), channel_id=1, source_target_pairs={{248,0},{0,8},{8,16},{16,24},{24,32},{32,40},{40,48},{48,56},{56,6... | collective-permute-start | bytes 6152 | tf_op jit(solution)/shard_map/while/body/eval_jaxpr/ppermute | solution.py:41
  226.7 12.2 %collective-permute-start = (bf16[512,256]{1,0:T(8,128)(2,1)S(1)}, bf16[512,256]{1,0:T(8,128)(2,1)S(1)}, u32[]{:S(2)}, u32[]{:S(2)}) collective-permute-start(bf16[512,256]{1,0:T(8,128)(2,1)S(1)} %get-tuple-element.702), channel_id=1, source_target_pairs={{248,0},{0,8},{8,16},{16,24},{24,32},{32,40},{40,48},{48,56},{56,6... | collective-permute-start | bytes 786440 | tf_op jit(solution)/shard_map/while/body/eval_jaxpr/ppermute | solution.py:41
  226.8 10.4 %collective-permute-start.1 = (s32[512]{0:T(512)S(1)}, s32[512]{0:T(512)S(1)}, u32[]{:S(2)}, u32[]{:S(2)}) collective-permute-start(s32[512]{0:T(512)S(1)} %get-tuple-element.703), channel_id=1, source_target_pairs={{248,0},{0,8},{8,16},{16,24},{24,32},{32,40},{40,48},{48,56},{56,6... | collective-permute-start | bytes 6152 | tf_op jit(solution)/shard_map/while/body/eval_jaxpr/ppermute | solution.py:41
  239.0 11.4 %collective-permute-start = (bf16[512,256]{1,0:T(8,128)(2,1)S(1)}, bf16[512,256]{1,0:T(8,128)(2,1)S(1)}, u32[]{:S(2)}, u32[]{:S(2)}) collective-permute-start(bf16[512,256]{1,0:T(8,128)(2,1)S(1)} %get-tuple-element.702), channel_id=1, source_target_pairs={{248,0},{0,8},{8,16},{16,24},{24,32},{32,40},{40,48},{48,56},{56,6... | collective-permute-start | bytes 786440 | tf_op jit(solution)/shard_map/while/body/eval_jaxpr/ppermute | solution.py:41
  239.1 9.5 %collective-permute-start.1 = (s32[512]{0:T(512)S(1)}, s32[512]{0:T(512)S(1)}, u32[]{:S(2)}, u32[]{:S(2)}) collective-permute-start(s32[512]{0:T(512)S(1)} %get-tuple-element.703), channel_id=1, source_target_pairs={{248,0},{0,8},{8,16},{16,24},{24,32},{32,40},{40,48},{48,56},{56,6... | collective-permute-start | bytes 6152 | tf_op jit(solution)/shard_map/while/body/eval_jaxpr/ppermute | solution.py:41
  250.5 11.4 %collective-permute-start = (bf16[512,256]{1,0:T(8,128)(2,1)S(1)}, bf16[512,256]{1,0:T(8,128)(2,1)S(1)}, u32[]{:S(2)}, u32[]{:S(2)}) collective-permute-start(bf16[512,256]{1,0:T(8,128)(2,1)S(1)} %get-tuple-element.702), channel_id=1, source_target_pairs={{248,0},{0,8},{8,16},{16,24},{24,32},{32,40},{40,48},{48,56},{56,6... | collective-permute-start | bytes 786440 | tf_op jit(solution)/shard_map/while/body/eval_jaxpr/ppermute | solution.py:41
  250.6 9.6 %collective-permute-start.1 = (s32[512]{0:T(512)S(1)}, s32[512]{0:T(512)S(1)}, u32[]{:S(2)}, u32[]{:S(2)}) collective-permute-start(s32[512]{0:T(512)S(1)} %get-tuple-element.703), channel_id=1, source_target_pairs={{248,0},{0,8},{8,16},{16,24},{24,32},{32,40},{40,48},{48,56},{56,6... | collective-permute-start | bytes 6152 | tf_op jit(solution)/shard_map/while/body/eval_jaxpr/ppermute | solution.py:41
  262.0 12.1 %collective-permute-start = (bf16[512,256]{1,0:T(8,128)(2,1)S(1)}, bf16[512,256]{1,0:T(8,128)(2,1)S(1)}, u32[]{:S(2)}, u32[]{:S(2)}) collective-permute-start(bf16[512,256]{1,0:T(8,128)(2,1)S(1)} %get-tuple-element.702), channel_id=1, source_target_pairs={{248,0},{0,8},{8,16},{16,24},{24,32},{32,40},{40,48},{48,56},{56,6... | collective-permute-start | bytes 786440 | tf_op jit(solution)/shard_map/while/body/eval_jaxpr/ppermute | solution.py:41
  274.2 14.6 %collective-permute-start = (bf16[512,256]{1,0:T(8,128)(2,1)S(1)}, bf16[512,256]{1,0:T(8,128)(2,1)S(1)}, u32[]{:S(2)}, u32[]{:S(2)}) collective-permute-start(bf16[512,256]{1,0:T(8,128)(2,1)S(1)} %get-tuple-element.702), channel_id=1, source_target_pairs={{248,0},{0,8},{8,16},{16,24},{24,32},{32,40},{40,48},{48,56},{56,6... | collective-permute-start | bytes 786440 | tf_op jit(solution)/shard_map/while/body/eval_jaxpr/ppermute | solution.py:41
  (20 other events, 212.4 us)
Sparse Core Ops, SparseCore 0:
  296.2 102.7 reduce-scatter.1
